TPU v7x, 256 devices: a whole 4x4x8 slice. The times are simulated.
256 devices in a mesh: facet: 64 (over z, y, core), freq: 4 (over x).
Axes of the slice: x: 4, y: 4, z: 8, core: 2. Of those that a mesh axis runs over, the one named last changes fastest.
Arguments:
- visibilities: bfloat16 [4, 16384, 2, 512], P('freq', 'facet'), may hold values from -6 to 6
- uvw: bfloat16 [4, 16384, 3, 512], P('freq', 'facet'), may hold values from -4 to 4
- facet_of: int32 [4, 16384, 1], P('freq', 'facet'), may hold values from 0 to 63; in each aligned block of 256 rows (0 to 255, 256 to 511, ..., all dimensions but the last counted through in order) at most 16 rows name the same one
- plane_of: int32 [4, 16384], P('freq', 'facet'), may hold values from 0 to 7
- cell_of: int32 [4, 16384], P('freq', 'facet'), may hold values from 0 to 1023
- kernels: bfloat16 [8, 2, 512, 256], replicated, may hold values from -0.25 to 0.25
- centers: float32 [64, 2], replicated, may hold values from -0.4 to 0.4
Outputs:
- images: float32 [64, 512, 512], P('facet', None, 'freq')
Inputs may be any that keep to these rules, and one draw needn't show every extreme that they name: `facet_of`: the facet index k is held by index k of the facet axis. In each aligned block of 256 tiles of one group, no facet is named by more than 16 tiles, and in some blocks one facet is named by exactly 16.
All inputs are finite; a program needn't handle non-finite values.
Results may differ from a plain program's by a relative error of at most 0.0095.
Values may be sent and summed in bfloat16 or wider, within the bound.
A program may use at most 128 MiB of HBM per device.

v0:
```python
import jax
import jax.numpy as jnp
from jax import lax
from jax.sharding import PartitionSpec as P

GRID = 512
PSIDE = 16


def split_up(shard, dim, devices):
    before, after = (shard.shape[:dim], shard.shape[dim + 1 :])
    return jnp.moveaxis(shard.reshape(*before, devices, -1, *after), dim, 0)


def summed_on_arrival(shard, axis, dim):
    devices = lax.axis_size(axis)
    blocks = lax.all_to_all(split_up(shard, dim, devices), axis, 0, 0, tiled=True)
    return jnp.sum(blocks.astype(jnp.float32), axis=0)


def dft_tables(length):
    indices = jnp.arange(length, dtype=jnp.int32)
    products_mod = indices[:, None] * indices[None, :] % length
    angle_table = products_mod.astype(jnp.float32) * (2.0 * jnp.pi / length)
    norm_scale = 1.0 / jnp.sqrt(jnp.float32(length))
    table_real = (jnp.cos(angle_table) * norm_scale).astype(jnp.bfloat16)
    table_imag = (jnp.sin(angle_table) * norm_scale).astype(jnp.bfloat16)
    return (table_real, table_imag)


def rotate_tiles(vis_pair, coords, sky_pos):
    l_coord = sky_pos[:, 0:1]
    m_coord = sky_pos[:, 1:2]
    w_term = jnp.sqrt(1.0 - l_coord * l_coord - m_coord * m_coord) - 1.0
    coords = coords.astype(jnp.float32)
    phase_angle = (
        2.0 * jnp.pi * (l_coord * coords[:, 0] + m_coord * coords[:, 1] + w_term * coords[:, 2])
    )
    cosine = jnp.cos(phase_angle)
    sine_part = jnp.sin(phase_angle)
    real_part = vis_pair[:, 0].astype(jnp.float32)
    imag_part = vis_pair[:, 1].astype(jnp.float32)
    rot_real = (real_part * cosine + imag_part * sine_part).astype(jnp.bfloat16)
    rot_imag = (imag_part * cosine - real_part * sine_part).astype(jnp.bfloat16)
    return (rot_real, rot_imag)


def stack_kernels(kernels):
    kern_real = kernels[:, 0]
    kern_imag = kernels[:, 1]
    upper_rows = jnp.concatenate([kern_real, kern_imag], axis=2)
    lower_rows = jnp.concatenate([-kern_imag, kern_real], axis=2)
    stacked_rows = jnp.concatenate([upper_rows, lower_rows], axis=0)
    return stacked_rows.reshape(-1, stacked_rows.shape[2])


def grid_tiles(rot_real, rot_imag, planes, stacked, plane_count):
    plane_select = (planes[:, None] == jnp.arange(plane_count)[None, :]).astype(jnp.bfloat16)
    spread = jnp.concatenate(
        [
            rot_real[:, None, :] * plane_select[:, :, None],
            rot_imag[:, None, :] * plane_select[:, :, None],
        ],
        axis=1,
    )
    spread = spread.reshape(spread.shape[0], -1)
    return jnp.dot(spread, stacked, preferred_element_type=jnp.float32).astype(jnp.bfloat16)


def shards(visibilities, uvw, facet_of, plane_of, cell_of, kernels, centers):
    peer_count = lax.axis_size("facet")
    tile_count = visibilities.shape[1]
    capacity = 4 * tile_count // peer_count
    total_slots = peer_count * capacity
    vis_pair = visibilities[0]
    coords = uvw[0]
    target = facet_of[0, :, 0]
    planes = plane_of[0]
    tile_cells = cell_of[0]
    plane_count = kernels.shape[0]
    stacked = stack_kernels(kernels)
    dest_hits = (target[:, None] == jnp.arange(peer_count)[None, :]).astype(jnp.int32)
    before = jnp.cumsum(dest_hits, axis=0) - dest_hits
    within_rank = jnp.sum(before * dest_hits, axis=1)
    slot_index = target * capacity + within_rank
    chosen = (target[:, None] == jnp.arange(centers.shape[0])[None, :]).astype(jnp.float32)
    sky_rows = jnp.sum(chosen[:, :, None] * centers[None, :, :], axis=1)
    rot_real, rot_imag = rotate_tiles(vis_pair, coords, sky_rows)
    own_patches = grid_tiles(rot_real, rot_imag, planes, stacked, plane_count)
    patch_buffer = (
        jnp.zeros((total_slots, own_patches.shape[1]), jnp.bfloat16).at[slot_index].set(own_patches)
    )
    cell_buffer = jnp.zeros((total_slots,), jnp.int32).at[slot_index].set(tile_cells)
    patches, slot_cells = (
        lax.all_to_all(
            patch_buffer.reshape(peer_count, capacity, -1),
            "facet",
            split_axis=0,
            concat_axis=0,
            tiled=True,
        ),
        lax.all_to_all(
            cell_buffer.reshape(peer_count, capacity),
            "facet",
            split_axis=0,
            concat_axis=0,
            tiled=True,
        ),
    )
    patches = patches.reshape(-1, patches.shape[-1])
    slot_cells = slot_cells.reshape(-1)
    nblocks = GRID // PSIDE
    ncells = nblocks * nblocks
    placing = (slot_cells[None, :] == jnp.arange(ncells)[:, None]).astype(jnp.bfloat16)
    blocks = jnp.dot(placing, patches, preferred_element_type=jnp.float32).astype(jnp.bfloat16)
    uv_grid = (
        blocks.reshape(nblocks, nblocks, 2, PSIDE, PSIDE)
        .transpose(2, 0, 3, 1, 4)
        .reshape(2 * GRID, GRID)
    )
    table_real, table_imag = dft_tables(GRID)
    table_both = jnp.concatenate([table_real, table_imag], axis=1)
    product = jnp.dot(uv_grid, table_both, preferred_element_type=jnp.float32)
    half_real = product[:GRID, :GRID] - product[GRID:, GRID:]
    half_imag = product[:GRID, GRID:] + product[GRID:, :GRID]
    partial_value = jnp.stack([half_real, half_imag]).astype(jnp.bfloat16)
    summed = summed_on_arrival(
        partial_value.astype(jnp.float32).astype(jnp.bfloat16), "freq", 2
    ).astype(jnp.bfloat16)
    right_side = jnp.concatenate([summed[0], -summed[1]], axis=0)
    facet_image = jnp.dot(table_both, right_side, preferred_element_type=jnp.float32)
    return facet_image[None]


def solution(mesh):
    in_specs = (
        P("freq", "facet", None, None),
        P("freq", "facet", None, None),
        P("freq", "facet", None),
        P("freq", "facet"),
        P("freq", "facet"),
        P(),
        P(),
    )
    out_specs = P("facet", None, "freq")
    return jax.shard_map(shards, mesh=mesh, in_specs=in_specs, out_specs=out_specs, check_vma=False)
```

profile of v0, /device:TPU:1, one launch (start us, length us, event | category | flops | bytes accessed | tf_op | source)
XLA Modules:
  0.0 122.2 jit_solution(14115856590694650843)
XLA Ops:
  0.0 0.7 fusion.52
  0.7 0.6 reduce-window.6
  1.5 0.8 fusion.50
  2.3 0.7 compare_select_fusion
  3.0 1.6 %scatter_custom_fusion = s32[1024]{0:T(1024)S(1)} fusion(s32[256]{0:T(256)S(1)} %bitcast.93, s32[256]{0:T(256)} %bitcast.95, s32[]{:T(128)} %constant.14.clone.1), kind=kCustom, calls=%fused_computation.82 | custom fusion | bytes 4608 | tf_op jit(solution)/shard_map/scatter | solution.py:93
  4.6 0.7 all_to_all.12
  5.3 13.1 %all-to-all-start = ((s32[64,1,16]{2,1,0:T(1,128)}), s32[64,1,16]{2,1,0:T(1,128)S(1)}, u32[]{:S(2)}, u32[]{:S(2)}) async-start(s32[64,1,16]{2,1,0:T(1,128)} %bitcast.7), calls=%async_computation | async-start | bytes 65536 | tf_op jit(solution)/shard_map/all_to_all | solution.py:102
  18.4 0.7 fusion.51
  19.1 2.7 %slice_bitcast_fusion = (bf16[8,512,256]{2,1,0:T(8,128)(2,1)S(1)}, bf16[8,512,256]{2,1,0:T(8,128)(2,1)S(1)}) fusion(bf16[8,2,512,256]{3,2,1,0:T(8,128)(2,1)} %param.12), kind=kLoop, calls=%fused_computation.15 | loop fusion | bytes 8388608 | tf_op jit(solution)/shard_map/squeeze | solution.py:50
  21.9 0.7 copy-done
  22.7 0.5 copy-done.3
  23.3 0.4 copy-done.1
  23.9 0.4 copy-done.2
  24.4 2.1 %fusion.60 = (f32[256,1,512]{2,0,1:T(8,128)S(1)}, f32[256,1,512]{2,0,1:T(8,128)S(1)}) fusion(f32[256,3,512]{2,0,1:T(8,128)S(1)} %bitcast_convert_fusion, f32[256]{0:T(256)S(1)} %bitcast.89, f32[256]{0:T(256)S(1)} %bitcast.90, f32[256]{0:T(256)S(1)} %bitcast.88), kind=kLoop, calls=%fused_computation.90 | loop fusion | flops 786432 | bytes 2624512 | tf_op jit(solution)/shard_map/cos | solution.py:39
  26.5 1.9 %fusion.43 = (bf16[256,512]{1,0:T(8,128)(2,1)S(1)}, bf16[256,512]{1,0:T(8,128)(2,1)S(1)}) fusion(f32[256,1,512]{2,0,1:T(8,128)S(1)} %get-tuple-element.5, bf16[256,2,512]{2,0,1:T(8,128)(2,1)S(1)} %bitcast.83, f32[256,1,512]{2,0,1:T(8,128)S(1)} %get-tuple-element.6), kind=kLoop, calls=%fused_computation.61 | loop fusion | flops 1310720 | bytes 2097152 | tf_op jit(solution)/shard_map/mul | solution.py:61
  28.4 0.4 broadcast_multiply_fusion.1
  28.9 2.3 %fusion.19 = bf16[256,512]{1,0:T(8,128)(2,1)S(1)} fusion(bf16[8,512,256]{2,1,0:T(8,128)(2,1)S(1)} %get-tuple-element.10, bf16[8,512,256]{2,1,0:T(8,128)(2,1)S(1)} %fusion.59, bf16[8,512,256]{2,1,0:T(8,128)(2,1)S(1)} %get-tuple-element.9, bf16[256,8,512]{2,0,1:T(8,128)(2,1)S(1)} %get-tuple-element.16, bf16[256,8,512]{2,0,1:T(8,128)(2,1)S(1)} %get-tuple-element.15), kind=kOutput, calls=%fused_computation.23 | convolution fusion | flops 2183266304 | bytes 10747904 | tf_op jit(solution)/shard_map/dot_general | solution.py:67
  31.2 2.6 %scatter_custom_fusion.1 = bf16[1024,512]{1,0:T(8,128)(2,1)} fusion(s32[256]{0:T(256)S(1)} %bitcast.94, bf16[256,512]{1,0:T(8,128)(2,1)S(1)} %fusion.19, bf16[]{:T(256)} %constant.36.clone.1), kind=kCustom, calls=%fused_computation.58 | custom fusion | bytes 1048578 | tf_op jit(solution)/shard_map/scatter | solution.py:91
  33.8 10.3 %all-to-all-start.1 = ((bf16[64,16,512]{2,1,0:T(8,128)(2,1)}), bf16[64,16,512]{2,1,0:T(8,128)(2,1)S(1)}, u32[]{:S(2)}, u32[]{:S(2)}) async-start(bf16[64,16,512]{2,1,0:T(8,128)(2,1)} %bitcast.20), calls=%async_computation.1 | async-start | bytes 2097152 | tf_op jit(solution)/shard_map/all_to_all | solution.py:95
  44.1 4.4 %multiply_convert_fusion = (bf16[512,512]{1,0:T(8,128)(2,1)S(1)}, bf16[512,512]{1,0:T(8,128)(2,1)S(1)}) fusion(), kind=kLoop, calls=%fused_computation.36 | loop fusion | flops 4718592 | bytes 1048576 | tf_op jit(solution)/shard_map/convert_element_type | solution.py:27
  48.5 0.5 broadcast.136
  49.1 0.7 reduce.6
  49.9 22.4 %all-to-all-done.1 = bf16[64,16,512]{2,1,0:T(8,128)(2,1)S(1)} async-done(((bf16[64,16,512]{2,1,0:T(8,128)(2,1)}), bf16[64,16,512]{2,1,0:T(8,128)(2,1)S(1)}, u32[]{:S(2)}, u32[]{:S(2)}) %all-to-all-start.1) | async-done | bytes 1048608 | tf_op jit(solution)/shard_map/all_to_all | solution.py:95
  72.3 1.3 %fusion.13 = bf16[1024,512]{1,0:T(8,128)(2,1)S(1)} fusion(bf16[1024,512]{1,0:T(8,128)(2,1)S(1)} %bitcast.84, s32[1024]{0:T(1024)S(1)} %eq.80), kind=kOutput, calls=%fused_computation.21 | convolution fusion | flops 1075314688 | bytes 2101248 | tf_op jit(solution)/shard_map/dot_general | solution.py:115
  73.6 0.5 copy.37
  74.1 4.4 %reshape.164 = bf16[32,32,2,16,16]{1,0,4,3,2:T(8,128)(2,1)} reshape(bf16[1024,512]{0,1:T(8,128)(2,1)S(1)} %copy.37) | data formatting | bytes 2097152 | tf_op jit(solution)/shard_map/reshape | solution.py:117
  78.5 8.8 %copy.38 = bf16[2,32,16,32,16]{4,3,2,1,0:T(8,128)(2,1)} copy(bf16[2,32,16,32,16]{3,1,4,2,0:T(8,128)(2,1)} %bitcast.80) | data formatting | bytes 2097152 | tf_op jit(solution)/shard_map/transpose | solution.py:118
  87.3 14.4 %reshape.165 = bf16[1024,512]{1,0:T(8,128)(2,1)S(1)} reshape(bf16[2,32,16,32,16]{4,3,2,1,0:T(8,128)(2,1)} %copy.38) | data formatting | bytes 2097152 | tf_op jit(solution)/shard_map/reshape | solution.py:119
  101.7 1.3 %fusion.32 = f32[1024,1024]{0,1:T(8,128)S(1)} fusion(bf16[1024,512]{1,0:T(8,128)(2,1)S(1)} %reshape.165, bf16[512,512]{1,0:T(8,128)(2,1)S(1)} %get-tuple-element.20, bf16[512,512]{1,0:T(8,128)(2,1)S(1)} %get-tuple-element.21), kind=kOutput, calls=%fused_computation.42 | convolution fusion | flops 1075838976 | bytes 6291456 | tf_op jit(solution)/shard_map/dot_general | solution.py:123
  103.0 0.4 fusion.28
  103.5 17.3 %all_to_all.19 = bf16[4,2,512,128]{2,3,1,0:T(8,128)(2,1)S(1)} all-to-all(bf16[4,2,512,128]{2,3,1,0:T(8,128)(2,1)S(1)} %maximum_bitcast_fusion), channel_id=1, replica_groups=mesh['facet'=64,'freq'=4] {'freq'}, dimensions={0} | all-to-all | bytes 2097152 | tf_op jit(solution)/shard_map/all_to_all | solution.py:17
  121.1 1.1 convolution_bitcast_fusion
  (20 shorter events, 1.2 us)
Async XLA Ops:
  5.3 28.6 %all-to-all-start = ((s32[64,1,16]{2,1,0:T(1,128)}), s32[64,1,16]{2,1,0:T(1,128)S(1)}, u32[]{:S(2)}, u32[]{:S(2)}) async-start(s32[64,1,16]{2,1,0:T(1,128)} %bitcast.7), calls=%async_computation | async-start | bytes 65536 | tf_op jit(solution)/shard_map/all_to_all | solution.py:102
  19.1 3.5 %copy-start = (bf16[8,2,512,256]{3,2,1,0:T(8,128)(2,1)S(1)}, bf16[8,2,512,256]{3,2,1,0:T(8,128)(2,1)}, u32[]{:S(2)}) copy-start(bf16[8,2,512,256]{3,2,1,0:T(8,128)(2,1)} %param.12) | copy-start | bytes 12582916
  22.5 0.7 copy-start.3
  22.5 1.1 copy-start.1
  23.2 1.1 copy-start.2
  23.2 1.2 copy-start.4
  33.8 38.5 %all-to-all-start.1 = ((bf16[64,16,512]{2,1,0:T(8,128)(2,1)}), bf16[64,16,512]{2,1,0:T(8,128)(2,1)S(1)}, u32[]{:S(2)}, u32[]{:S(2)}) async-start(bf16[64,16,512]{2,1,0:T(8,128)(2,1)} %bitcast.20), calls=%async_computation.1 | async-start | bytes 2097152 | tf_op jit(solution)/shard_map/all_to_all | solution.py:95
where the time goes:
time: 123 us; the launch traced here: 122 us
  local copies, waits for them, and re-layouts  38.6 us (31%)
  starting transfers between devices  23.4 us (19%)
  waiting for transfers between devices  22.4 us (18%)
  blocking collectives  17.3 us (14%)
  other arithmetic  14.2 us (12%)
  matrix products  6.02 us (5%)
    all_to_all x1, waiting for transfers between devices, shards(): lax.all_to_all(patch_buffer.reshape(peer_count, capacity, -1), 'facet', s...  22.4 us
    all_to_all x1, blocking collectives, summed_on_arrival(): lax.all_to_all(split_up(shard, dim, devices), axis, 0, 0, tiled=True)  17.3 us
    reshape x1, local copies, waits for them, and re-layouts, shards(): uv_grid = blocks.reshape(nblocks, nblocks, 2, PSIDE, PSIDE).transpose(2,...  14.4 us
    all_to_all x1, starting transfers between devices, shards(): lax.all_to_all(cell_buffer.reshape(peer_count, capacity), 'facet', split_...  13.1 us
    all_to_all x1, starting transfers between devices, shards(): lax.all_to_all(patch_buffer.reshape(peer_count, capacity, -1), 'facet', s...  10.3 us
    transpose x1, local copies, waits for them, and re-layouts, shards(): uv_grid = blocks.reshape(nblocks, nblocks, 2, PSIDE, PSIDE).transpose(2,...  8.76 us
    reshape x1, local copies, waits for them, and re-layouts, shards(): blocks.reshape(nblocks, nblocks, 2, PSIDE, PSIDE).transpose(2, 0, 3, 1, 4)  4.4 us
    convert_element_type x1, other arithmetic, dft_tables(): table_imag = (jnp.sin(angle_table) * norm_scale).astype(jnp.bfloat16)  4.39 us
  transfers between devices with their start and end apart: 2, of which 1 were waited for; matrix products, arithmetic and copies ran while one was open for 16% of the time, Pallas kernels for 0%

commit v1 on v0

v1 whole, which is shorter than its diff:
```python
import functools

import jax
import jax.numpy as jnp
import numpy as np
from jax import lax
from jax.experimental import pallas as pl
from jax.experimental.pallas import tpu as pltpu
from jax.sharding import PartitionSpec as P

MESH = pl.DeviceIdType.MESH
F32, BF16 = jnp.float32, jnp.bfloat16
SLOTS = 16
PU_SETS = ((0, 8, 4, 12), (1, 15, 7, 9), (2, 14, 6, 10), (3, 13, 5, 11))
CHUNKS = 4
SINE = (6.283185159611163, -41.34165492934347, 81.60099819261225, -76.54965682060198, 39.53581371130458)


def constants():
    perm = np.zeros((512, 512))
    twist = np.zeros((CHUNKS, 2, 32, 128))
    mix = np.zeros((CHUNKS, 64, 256))
    last = np.zeros((4, 16, CHUNKS, 4, 4, 4))
    ones = np.arange(32)
    pv = np.arange(16)
    j2 = np.arange(16)
    for h, pus in enumerate(PU_SETS):
        for i, pu in enumerate(pus):
            for c in range(2):
                for v in range(16):
                    perm[c * 256 + pu * 16 + v, h * 128 + c * 64 + i * 16 + v] = 1
                angle = 2 * np.pi * pu * ones / 512
                lanes = slice(c * 64 + i * 16, c * 64 + i * 16 + 16)
                twist[h, 0, :, lanes] = np.cos(angle)[:, None]
                twist[h, 1, :, lanes] = np.sin(angle)[:, None]
        if h == 0:
            outputs = [((0, 1, 0),), ((1, 1, 0),), ((2, 1, 0), (3, 1, 0)), ((2, 0, 1), (3, 0, -1))]
            weights = [np.ones(16), np.cos(np.pi * j2), np.cos(2 * np.pi * 4 * j2 / 16), -np.sin(2 * np.pi * 4 * j2 / 16)]
        else:
            outputs = [((0, 1, 0), (1, 1, 0)), ((0, 0, 1), (1, 0, -1)), ((2, 1, 0), (3, 1, 0)), ((2, 0, 1), (3, 0, -1))]
            weights = []
            for a in (pus[0], pus[2]):
                weights += [np.cos(2 * np.pi * a * j2 / 16), -np.sin(2 * np.pi * a * j2 / 16)]
        for o in range(4):
            for k2 in range(16):
                row = (k2 // 4) * 16 + o * 4 + k2 % 4
                cos, sin = np.cos(2 * np.pi * pv * k2 / 16), np.sin(2 * np.pi * pv * k2 / 16)
                for i, re, im in outputs[o]:
                    on_re = re * cos + im * sin
                    on_im = -re * sin + im * cos
                    at = i * 16
                    mix[h, row, at : at + 16] += on_re
                    mix[h, row, 64 + at : 64 + at + 16] += on_im
                    mix[h, row, 128 + at : 128 + at + 16] += on_im
                    mix[h, row, 192 + at : 192 + at + 16] -= on_re
            for k in range(4):
                last[k, :, h, :, o, k] = (weights[o] / 512)[:, None]
    inner = 2 * np.pi * ones[:, None] * np.tile(pv, 8)[None, :] / 512
    inner = np.stack([np.cos(inner), np.sin(inner)])
    return (
        perm.astype(BF16),
        twist.astype(np.float32),
        inner.astype(np.float32),
        mix.astype(BF16),
        last.reshape(64, 256).astype(BF16),
    )


def sine(turns):
    turns = turns - 0.25
    turns = turns - jnp.floor(turns + 0.5)
    y = 0.25 - jnp.abs(turns)
    y2 = y * y
    total = F32(SINE[4])
    for c in SINE[3::-1]:
        total = total * y2 + F32(c)
    return total * y


def cosine(turns):
    return sine(turns + 0.25)


def iota(shape, dim, kind=jnp.int32):
    return lax.broadcasted_iota(jnp.int32, shape, dim).astype(kind)


def dot(a, b):
    return jnp.dot(a, b, preferred_element_type=F32)


def dot_nt(a, b):
    return lax.dot_general(a, b, (((1,), (1,)), ((), ())), preferred_element_type=F32)


def kernel(peers, groups, vis, uvw, fac, pla, cel, ker, cen, perm, twist, inner, mix, last, out,
           k_v, cols, lhs, send, recv, csend, crecv, ucs, left, xy, pq, xsend, xrecv,
           ksem, ssem, rsem, cssem, crsem, xssem, xrsem):
    me = lax.axis_index("facet")
    fq = lax.axis_index("freq")

    barrier = pltpu.get_barrier_semaphore()

    @pl.loop(1, peers)
    def _(i):
        pl.semaphore_signal(barrier, inc=1, device_id={"facet": lax.rem(me + i, peers)}, device_id_type=MESH)

    @pl.loop(1, groups)
    def _(i):
        pl.semaphore_signal(barrier, inc=1, device_id={"freq": lax.rem(fq + i, groups)}, device_id_type=MESH)

    loads = []
    for p in range(8):
        for c in range(2):
            copy = pltpu.make_async_copy(ker.at[p, c], k_v.at[pl.ds(512 * p, 512), pl.ds(256 * c, 256)], ksem)
            copy.start()
            loads.append(copy)

    target = fac[...]
    dest = (iota((64, 256), 0) == target)
    dest_b = dest.astype(F32).astype(BF16)
    tri = (iota((256, 256), 0) < iota((256, 256), 1)).astype(F32).astype(BF16)
    before = dot(dest_b, tri)
    rank = jnp.sum(jnp.where(dest, before, 0.0), axis=0, keepdims=True).astype(jnp.int32)
    slot = target * SLOTS + rank

    cells = cel[...]
    spot = lax.rem(me, 8) * SLOTS + rank
    here = iota((128, 256), 0) == spot
    high = jnp.where(here, (cells // 32).astype(F32), 0.0).astype(BF16)
    low = jnp.where(here, lax.rem(cells, 32).astype(F32), 0.0).astype(BF16)
    rows = dot_nt(dest_b, high) * 32.0 + dot_nt(dest_b, low)
    csend[...] = rows.reshape(64, 1, 128)

    eye = iota((256, 256), 0) == iota((256, 256), 1)
    target_col = jnp.sum(jnp.where(eye, target.astype(F32), 0.0), axis=1, keepdims=True)
    plane_col = jnp.sum(jnp.where(eye, pla[...].astype(F32), 0.0), axis=1, keepdims=True)
    mine = target_col == iota((256, 64), 1, F32)
    l_col = jnp.sum(jnp.where(mine, cen[0:1, :], 0.0), axis=1, keepdims=True)
    m_col = jnp.sum(jnp.where(mine, cen[1:2, :], 0.0), axis=1, keepdims=True)
    l_all = jnp.broadcast_to(l_col, (256, 128))
    m_all = jnp.broadcast_to(m_col, (256, 128))
    cols[0] = l_all
    cols[1] = m_all
    cols[2] = jnp.sqrt(1.0 - l_all * l_all - m_all * m_all) - 1.0
    cols[3] = jnp.broadcast_to(plane_col, (256, 128))

    @pl.loop(0, 16)
    def _(b):
        at = pl.ds(pl.multiple_of(b * 16, 16), 16)

        def wide(n):
            return jnp.concatenate([cols[n, at, :]] * 4, axis=1)

        turns = wide(0) * uvw[0, at, :].astype(F32) + wide(1) * uvw[1, at, :].astype(F32) + wide(2) * uvw[2, at, :].astype(F32)
        cos, sin = cosine(turns), sine(turns)
        re, im = vis[0, at, :].astype(F32), vis[1, at, :].astype(F32)
        new_re = (re * cos + im * sin).astype(BF16)
        new_im = (im * cos - re * sin).astype(BF16)
        plane = wide(3)
        lower = pl.ds(pl.multiple_of(b * 16 + 256, 16), 16)
        for p in range(8):
            keep = (plane == p).astype(F32).astype(BF16)
            lhs[at, 512 * p : 512 * p + 512] = new_re * keep
            lhs[lower, 512 * p : 512 * p + 512] = new_im * keep

    for copy in loads:
        copy.wait()
    with_re = dot(lhs[...], k_v[:, :256])
    with_im = dot(lhs[...], k_v[:, 256:])
    patch = jnp.concatenate([with_re[:256] - with_im[256:], with_im[:256] + with_re[256:]], axis=1).astype(BF16)
    patch = dot(patch, perm[...]).astype(BF16)
    pick = (iota((1024, 256), 0) == slot).astype(F32).astype(BF16)

    pl.semaphore_wait(barrier, peers - 1 + groups - 1)

    @pl.loop(1, peers)
    def _(i):
        d = lax.rem(me + i, peers)
        pltpu.make_async_remote_copy(csend.at[d], crecv.at[me], cssem, crsem, device_id={"facet": d}, device_id_type=MESH).start()

    for h in range(CHUNKS):
        block = dot(pick, patch[:, 128 * h : 128 * h + 128]).astype(BF16)
        send[h] = block.reshape(64, SLOTS, 128)

        @pl.loop(1, peers)
        def _(i):
            d = lax.rem(me + i, peers)
            pltpu.make_async_remote_copy(send.at[h, d], recv.at[h, me], ssem, rsem.at[h], device_id={"facet": d}, device_id_type=MESH).start()

        recv[h, me] = send[h, me]
    crecv[me] = csend[me]

    some = pl.ds(0, peers - 1)
    pltpu.make_async_copy(csend.at[some], crecv.at[some], crsem).wait()
    for g in range(8):
        cell = jnp.sum(crecv[8 * g : 8 * g + 8], axis=0)
        bu = jnp.floor(cell * (1.0 / 32.0))
        bv = cell - 32.0 * bu
        lanes = slice(128 * g, 128 * g + 128)
        count = iota((32, 128), 0, F32) * (1.0 / 32.0)
        for n, turns in enumerate((count * bu, count * bv)):
            ucs[2 * n, :, lanes] = cosine(turns)
            ucs[2 * n + 1, :, lanes] = sine(turns)

    @pl.loop(0, 32)
    def _(j):
        uc, us = ucs[0, pl.ds(j, 1), :], ucs[1, pl.ds(j, 1), :]
        vc, vs = ucs[2], ucs[3]
        left[pl.ds(pl.multiple_of(j * 32, 32), 32), :] = (uc * vc - us * vs).astype(BF16)
        left[pl.ds(pl.multiple_of(j * 32 + 1024, 32), 32), :] = (us * vc + uc * vs).astype(BF16)

    for h in range(CHUNKS):
        pltpu.make_async_copy(send.at[h, some], recv.at[h, some], rsem.at[h]).wait()
        xy[...] = dot(left[...], recv[h].reshape(1024, 128))
        ec, es = inner[0], inner[1]

        @pl.loop(0, 32)
        def _(j):
            at = pl.ds(pl.multiple_of(j * 32, 32), 32)
            x, y = xy[at, :], xy[pl.ds(pl.multiple_of(j * 32 + 1024, 32), 32), :]
            dc, ds = twist[h, 0, pl.ds(j, 1), :], twist[h, 1, pl.ds(j, 1), :]
            tc, ts = dc * ec - ds * es, ds * ec + dc * es
            pq[at, 0:128] = (x * tc - y * ts).astype(BF16)
            pq[at, 128:256] = (y * tc + x * ts).astype(BF16)

        xsend[h] = dot_nt(mix[h], pq[...]).astype(BF16).reshape(4, 16, 1024)

        @pl.loop(1, groups)
        def _(i):
            d = lax.rem(fq + i, groups)
            pltpu.make_async_remote_copy(xsend.at[h, d], xrecv.at[h, fq], xssem, xrsem.at[h], device_id={"freq": d}, device_id_type=MESH).start()

        xrecv[h, fq] = xsend[h, fq]

    for h in range(CHUNKS):
        few = pl.ds(0, groups - 1)
        pltpu.make_async_copy(xsend.at[h, few], xrecv.at[h, few], xrsem.at[h]).wait()
    image = dot(last[...], xrecv[...].reshape(256, 1024))
    for a in range(32):
        out[:, a, :] = jnp.concatenate([image[16 * k : 16 * k + 16, 32 * a : 32 * a + 32] for k in range(4)], axis=1)

    pltpu.make_async_copy(csend.at[some], crecv.at[some], cssem).wait()
    for h in range(CHUNKS):
        pltpu.make_async_copy(send.at[h, some], recv.at[h, some], ssem).wait()
        few = pl.ds(0, groups - 1)
        pltpu.make_async_copy(xsend.at[h, few], xrecv.at[h, few], xssem).wait()


def solution(mesh):
    peers, groups = mesh.shape["facet"], mesh.shape["freq"]
    consts = constants()

    def shards(visibilities, uvw, facet_of, plane_of, cell_of, kernels, centers):
        vis = jnp.transpose(visibilities[0], (1, 0, 2))
        coords = jnp.transpose(uvw[0], (1, 0, 2))
        vmem = pl.BlockSpec(memory_space=pltpu.VMEM)
        dma = pltpu.SemaphoreType.DMA
        image = pl.pallas_call(
            functools.partial(kernel, peers, groups),
            out_shape=jax.ShapeDtypeStruct((16, 32, 128), F32),
            in_specs=[vmem] * 5 + [pl.BlockSpec(memory_space=pl.ANY)] + [vmem] * 6,
            out_specs=vmem,
            scratch_shapes=[
                pltpu.VMEM((4096, 512), BF16),
                pltpu.VMEM((4, 256, 128), F32),
                pltpu.VMEM((512, 4096), BF16),
                pltpu.VMEM((CHUNKS, 64, SLOTS, 128), BF16),
                pltpu.VMEM((CHUNKS, 64, SLOTS, 128), BF16),
                pltpu.VMEM((64, 1, 128), F32),
                pltpu.VMEM((64, 1, 128), F32),
                pltpu.VMEM((4, 32, 1024), F32),
                pltpu.VMEM((2048, 1024), BF16),
                pltpu.VMEM((2048, 128), F32),
                pltpu.VMEM((1024, 256), BF16),
                pltpu.VMEM((CHUNKS, 4, 16, 1024), BF16),
                pltpu.VMEM((CHUNKS, 4, 16, 1024), BF16),
                dma, dma, dma((CHUNKS,)), dma, dma, dma, dma((CHUNKS,)),
            ],
            compiler_params=pltpu.CompilerParams(collective_id=0, has_side_effects=True),
        )(vis, coords, facet_of.reshape(1, -1), plane_of, cell_of, kernels, centers.T, *[jnp.asarray(c) for c in consts])
        return image.reshape(1, 512, 128)

    in_specs = (
        P("freq", "facet", None, None),
        P("freq", "facet", None, None),
        P("freq", "facet", None),
        P("freq", "facet"),
        P("freq", "facet"),
        P(),
        P(),
    )
    return jax.shard_map(shards, mesh=mesh, in_specs=in_specs, out_specs=P("facet", None, "freq"), check_vma=False)
```

time: 123 us -> 57.2 us (0.47)
  Pallas kernels: 0 us -> 53.4 us
  local copies, waits for them, and re-layouts: 38.6 us -> 3.55 us
  starting transfers between devices: 23.4 us -> 0 us
  waiting for transfers between devices: 22.4 us -> 0 us
  blocking collectives: 17.3 us -> 0 us
  other arithmetic: 14.2 us -> 0 us
  matrix products: 6.02 us -> 0 us
    pallas_call x0 -> x1, Pallas kernels: none -> 53.4 us  [shards(): pl.pallas_call(functools.partial(kernel, peers, groups), out_shape=jax.Sh...]
    all_to_all x2 -> x0, starting transfers between devices: 23.4 us -> none  [the longest x1 13.1 us: shards(): lax.all_to_all(cell_buffer.reshape(peer_count, capacity), 'facet', split_...]
    all_to_all x2 -> x0, waiting for transfers between devices: 22.4 us -> none  [the longest x1 22.4 us: shards(): lax.all_to_all(patch_buffer.reshape(peer_count, capacity, -1), 'facet', s...]
    reshape x2 -> x0, local copies, waits for them, and re-layouts: 18.8 us -> none  [the longest x1 14.4 us: shards(): uv_grid = blocks.reshape(nblocks, nblocks, 2, PSIDE, PSIDE).transpose(2,...]
    all_to_all x1 -> x0, blocking collectives: 17.3 us -> none  [summed_on_arrival(): lax.all_to_all(split_up(shard, dim, devices), axis, 0, 0, tiled=True)]
    transpose x1 -> x0, local copies, waits for them, and re-layouts: 8.76 us -> none  [shards(): uv_grid = blocks.reshape(nblocks, nblocks, 2, PSIDE, PSIDE).transpose(2,...]
    dot_general x4 -> x0, matrix products: 6.02 us -> none  [the longest x1 2.32 us: grid_tiles(): jnp.dot(spread, stacked, preferred_element_type=jnp.float32)]
    convert_element_type x5 -> x0, other arithmetic: 5.97 us -> none  [the longest x1 4.39 us: dft_tables(): table_imag = (jnp.sin(angle_table) * norm_scale).astype(jnp.bfloat16)]
  transfers between devices with their start and end apart: 2 -> 0, of which waited for: 1 -> 0; matrix products, arithmetic and copies ran while one was open for 16% -> 0% of each run, Pallas kernels for 0% -> 0%
where the time goes in v1:
time: 57.2 us; the launch traced here: 57 us
  Pallas kernels  53.4 us (93%)
  local copies, waits for them, and re-layouts  3.55 us (6%)
    pallas_call x1, Pallas kernels, shards(): pl.pallas_call(functools.partial(kernel, peers, groups), out_shape=jax.Sh...  53.4 us
    unnamed x2, local copies, waits for them, and re-layouts  3.55 us

profile of v1, /device:TPU:1, one launch (start us, length us, event | category | flops | bytes accessed | tf_op | source)
XLA Modules:
  0.0 57.0 jit_solution(4336357528025178274)
XLA Ops:
  0.0 1.9 %copy.15 = bf16[1,256,2,512]{3,1,2,0:T(8,128)(2,1)} copy(bf16[1,256,2,512]{3,2,1,0:T(2,128)(2,1)} %param.12) | data formatting | bytes 1048576 | tf_op args[0]
  1.9 53.4 %shard_map.118 = f32[16,32,128]{2,1,0:T(8,128)} custom-call(bf16[2,256,512]{2,1,0:T(8,128)(2,1)} %bitcast.11, bf16[3,256,512]{2,1,0:T(8,128)(2,1)} %bitcast.13, s32[1,256]{1,0:T(1,128)} %bitcast.14, s32[1,256]{1,0:T(1,128)} %pla.1, s32[1,256]{1,0:T(1,128)} %cel.1, bf16[8,2,512,256]{3,2,1,0:T(8,128)(2,1)} %ker.1, f32[2,64]{1,0:T(2,128)} %bitcast.15, ...), custom_call_target="tpu_custom_call" | custom-call | tf_op jit(solution)/shard_map/pallas_call | solution.py:259
  55.3 1.7 %copy.17 = f32[1,512,128]{2,1,0:T(8,128)} copy(f32[1,512,128]{2,1,0:T(8,128)} %bitcast.12) | data formatting | bytes 524288

commit v2 on v1

--- a/solution.py
+++ b/solution.py
@@ -12,15 +12,18 @@
 F32, BF16 = jnp.float32, jnp.bfloat16
 SLOTS = 16
 PU_SETS = ((0, 8, 4, 12), (1, 15, 7, 9), (2, 14, 6, 10), (3, 13, 5, 11))
-CHUNKS = 4
+SETS = 4
+CHUNKS = ((0,), (1,), (2,), (3,))
+AHEAD = 2
+ROWS = 512
 SINE = (6.283185159611163, -41.34165492934347, 81.60099819261225, -76.54965682060198, 39.53581371130458)
 
 
 def constants():
     perm = np.zeros((512, 512))
-    twist = np.zeros((CHUNKS, 2, 32, 128))
-    mix = np.zeros((CHUNKS, 64, 256))
-    last = np.zeros((4, 16, CHUNKS, 4, 4, 4))
+    twist = np.zeros((SETS, 2, 32, 128))
+    mix = np.zeros((SETS, 64, 256))
+    last = np.zeros((4, 16, SETS, 4, 4))
     ones = np.arange(32)
     pv = np.arange(16)
     j2 = np.arange(16)
@@ -54,7 +57,9 @@
                     mix[h, row, 128 + at : 128 + at + 16] += on_im
                     mix[h, row, 192 + at : 192 + at + 16] -= on_re
             for k in range(4):
-                last[k, :, h, :, o, k] = (weights[o] / 512)[:, None]
+                last[k, :, h, o, k] = weights[o] / 512
+    last = last.reshape(64, SETS, 16)
+    last = [np.tile(last[:, list(sets)].reshape(64, -1), (1, 4)) for sets in CHUNKS]
     inner = 2 * np.pi * ones[:, None] * np.tile(pv, 8)[None, :] / 512
     inner = np.stack([np.cos(inner), np.sin(inner)])
     return (
@@ -62,7 +67,7 @@
         twist.astype(np.float32),
         inner.astype(np.float32),
         mix.astype(BF16),
-        last.reshape(64, 256).astype(BF16),
+        np.concatenate(last, axis=1).astype(BF16),
     )
 
 
@@ -93,28 +98,38 @@
     return lax.dot_general(a, b, (((1,), (1,)), ((), ())), preferred_element_type=F32)
 
 
-def kernel(peers, groups, vis, uvw, fac, pla, cel, ker, cen, perm, twist, inner, mix, last, out,
-           k_v, cols, lhs, send, recv, csend, crecv, ucs, left, xy, pq, xsend, xrecv,
-           ksem, ssem, rsem, cssem, crsem, xssem, xrsem):
+def kernel(peers, groups, *refs):
+    far, out, near, refs = refs[:12], refs[12], refs[13:24], refs[24:]
+    ker = far[11]
+    fac, pla, cel, cen, uvw, vis, perm, twist, inner, mix, last = near
+    k_v, cols, lhs, csend, crecv, ucs, left, pq, lsem, ksem, cssem, crsem, *rest = refs
+    n = len(CHUNKS)
+    send, recv, xsend, xrecv = (rest[n * i : n * i + n] for i in range(4))
+    ssem, rsem, xssem, xrsem, table = rest[4 * n :]
     me = lax.axis_index("facet")
     fq = lax.axis_index("freq")
 
-    barrier = pltpu.get_barrier_semaphore()
-
-    @pl.loop(1, peers)
-    def _(i):
-        pl.semaphore_signal(barrier, inc=1, device_id={"facet": lax.rem(me + i, peers)}, device_id_type=MESH)
-
-    @pl.loop(1, groups)
-    def _(i):
-        pl.semaphore_signal(barrier, inc=1, device_id={"freq": lax.rem(fq + i, groups)}, device_id_type=MESH)
-
+    arrive = [pltpu.make_async_copy(a, b, lsem.at[i]) for i, (a, b) in enumerate(zip(far, near))]
+    for copy in arrive:
+        copy.start()
     loads = []
     for p in range(8):
         for c in range(2):
             copy = pltpu.make_async_copy(ker.at[p, c], k_v.at[pl.ds(512 * p, 512), pl.ds(256 * c, 256)], ksem)
             copy.start()
             loads.append(copy)
+    barrier = pltpu.get_barrier_semaphore()
+
+    @pl.loop(1, peers)
+    def _(i):
+        pl.semaphore_signal(barrier, inc=1, device_id={"facet": lax.rem(me + i, peers)}, device_id_type=MESH)
+
+    @pl.loop(1, groups)
+    def _(i):
+        pl.semaphore_signal(barrier, inc=1, device_id={"freq": lax.rem(fq + i, groups)}, device_id_type=MESH)
+
+    for copy in arrive[:4]:
+        copy.wait()
 
     target = fac[...]
     dest = (iota((64, 256), 0) == target)
@@ -145,6 +160,9 @@
     cols[2] = jnp.sqrt(1.0 - l_all * l_all - m_all * m_all) - 1.0
     cols[3] = jnp.broadcast_to(plane_col, (256, 128))
 
+    arrive[4].wait()
+    arrive[5].wait()
+
     @pl.loop(0, 16)
     def _(b):
         at = pl.ds(pl.multiple_of(b * 16, 16), 16)
@@ -154,7 +172,8 @@
 
         turns = wide(0) * uvw[0, at, :].astype(F32) + wide(1) * uvw[1, at, :].astype(F32) + wide(2) * uvw[2, at, :].astype(F32)
         cos, sin = cosine(turns), sine(turns)
-        re, im = vis[0, at, :].astype(F32), vis[1, at, :].astype(F32)
+        both = vis[at].astype(F32)
+        re, im = both[:, 0, :], both[:, 1, :]
         new_re = (re * cos + im * sin).astype(BF16)
         new_im = (im * cos - re * sin).astype(BF16)
         plane = wide(3)
@@ -164,7 +183,14 @@
             lhs[at, 512 * p : 512 * p + 512] = new_re * keep
             lhs[lower, 512 * p : 512 * p + 512] = new_im * keep
 
-    for copy in loads:
+    pl.semaphore_wait(barrier, peers - 1 + groups - 1)
+
+    @pl.loop(1, peers)
+    def _(i):
+        d = lax.rem(me + i, peers)
+        pltpu.make_async_remote_copy(csend.at[d], crecv.at[me], cssem, crsem, device_id={"facet": d}, device_id_type=MESH).start()
+
+    for copy in arrive[6:] + loads:
         copy.wait()
     with_re = dot(lhs[...], k_v[:, :256])
     with_im = dot(lhs[...], k_v[:, 256:])
@@ -172,23 +198,20 @@
     patch = dot(patch, perm[...]).astype(BF16)
     pick = (iota((1024, 256), 0) == slot).astype(F32).astype(BF16)
 
-    pl.semaphore_wait(barrier, peers - 1 + groups - 1)
-
-    @pl.loop(1, peers)
-    def _(i):
-        d = lax.rem(me + i, peers)
-        pltpu.make_async_remote_copy(csend.at[d], crecv.at[me], cssem, crsem, device_id={"facet": d}, device_id_type=MESH).start()
-
-    for h in range(CHUNKS):
-        block = dot(pick, patch[:, 128 * h : 128 * h + 128]).astype(BF16)
-        send[h] = block.reshape(64, SLOTS, 128)
+    def launch(h):
+        for i, a in enumerate(CHUNKS[h]):
+            block = dot(pick, patch[:, 128 * a : 128 * a + 128]).astype(BF16)
+            send[h][:, :, 128 * i : 128 * i + 128] = block.reshape(64, SLOTS, 128)
 
         @pl.loop(1, peers)
         def _(i):
             d = lax.rem(me + i, peers)
-            pltpu.make_async_remote_copy(send.at[h, d], recv.at[h, me], ssem, rsem.at[h], device_id={"facet": d}, device_id_type=MESH).start()
-
-        recv[h, me] = send[h, me]
+            pltpu.make_async_remote_copy(send[h].at[d], recv[h].at[me], ssem.at[h], rsem.at[h], device_id={"facet": d}, device_id_type=MESH).start()
+
+        recv[h][me] = send[h][me]
+
+    for h in range(AHEAD):
+        launch(h)
     crecv[me] = csend[me]
 
     some = pl.ds(0, peers - 1)
@@ -199,9 +222,9 @@
         bv = cell - 32.0 * bu
         lanes = slice(128 * g, 128 * g + 128)
         count = iota((32, 128), 0, F32) * (1.0 / 32.0)
-        for n, turns in enumerate((count * bu, count * bv)):
-            ucs[2 * n, :, lanes] = cosine(turns)
-            ucs[2 * n + 1, :, lanes] = sine(turns)
+        for w, turns in enumerate((count * bu, count * bv)):
+            ucs[2 * w, :, lanes] = cosine(turns)
+            ucs[2 * w + 1, :, lanes] = sine(turns)
 
     @pl.loop(0, 32)
     def _(j):
@@ -210,75 +233,88 @@
         left[pl.ds(pl.multiple_of(j * 32, 32), 32), :] = (uc * vc - us * vs).astype(BF16)
         left[pl.ds(pl.multiple_of(j * 32 + 1024, 32), 32), :] = (us * vc + uc * vs).astype(BF16)
 
-    for h in range(CHUNKS):
-        pltpu.make_async_copy(send.at[h, some], recv.at[h, some], rsem.at[h]).wait()
-        xy[...] = dot(left[...], recv[h].reshape(1024, 128))
-        ec, es = inner[0], inner[1]
+    ec, es = inner[0], inner[1]
+    for a in range(SETS):
 
         @pl.loop(0, 32)
         def _(j):
             at = pl.ds(pl.multiple_of(j * 32, 32), 32)
-            x, y = xy[at, :], xy[pl.ds(pl.multiple_of(j * 32 + 1024, 32), 32), :]
-            dc, ds = twist[h, 0, pl.ds(j, 1), :], twist[h, 1, pl.ds(j, 1), :]
-            tc, ts = dc * ec - ds * es, ds * ec + dc * es
-            pq[at, 0:128] = (x * tc - y * ts).astype(BF16)
-            pq[at, 128:256] = (y * tc + x * ts).astype(BF16)
-
-        xsend[h] = dot_nt(mix[h], pq[...]).astype(BF16).reshape(4, 16, 1024)
+            dc, ds = twist[a, 0, pl.ds(j, 1), :], twist[a, 1, pl.ds(j, 1), :]
+            table[2 * a, at] = dc * ec - ds * es
+            table[2 * a + 1, at] = ds * ec + dc * es
+
+    for h, sets in enumerate(CHUNKS):
+        pltpu.make_async_copy(send[h].at[some], recv[h].at[some], rsem.at[h]).wait()
+        if h + AHEAD < n:
+            launch(h + AHEAD)
+        for i, a in enumerate(sets):
+            block = recv[h][:, :, 128 * i : 128 * i + 128].reshape(1024, 128)
+            for b in range(0, 1024, ROWS):
+                at = slice(b, b + ROWS)
+                x, y = dot(left[at], block), dot(left[b + 1024 : b + 1024 + ROWS], block)
+                tc, ts = table[2 * a, at], table[2 * a + 1, at]
+                pq[at, 0:128] = (x * tc - y * ts).astype(BF16)
+                pq[at, 128:256] = (y * tc + x * ts).astype(BF16)
+
+            xsend[h][:, 16 * i : 16 * i + 16, :] = dot_nt(mix[a], pq[...]).astype(BF16).reshape(4, 16, 1024)
 
         @pl.loop(1, groups)
         def _(i):
             d = lax.rem(fq + i, groups)
-            pltpu.make_async_remote_copy(xsend.at[h, d], xrecv.at[h, fq], xssem, xrsem.at[h], device_id={"freq": d}, device_id_type=MESH).start()
-
-        xrecv[h, fq] = xsend[h, fq]
-
-    for h in range(CHUNKS):
-        few = pl.ds(0, groups - 1)
-        pltpu.make_async_copy(xsend.at[h, few], xrecv.at[h, few], xrsem.at[h]).wait()
-    image = dot(last[...], xrecv[...].reshape(256, 1024))
+            pltpu.make_async_remote_copy(xsend[h].at[d], xrecv[h].at[fq], xssem.at[h], xrsem.at[h], device_id={"freq": d}, device_id_type=MESH).start()
+
+        xrecv[h][fq] = xsend[h][fq]
+
+    few = pl.ds(0, groups - 1)
+    image = 0.0
+    start = 0
+    for h, sets in enumerate(CHUNKS):
+        pltpu.make_async_copy(xsend[h].at[few], xrecv[h].at[few], xrsem.at[h]).wait()
+        wide = 64 * len(sets)
+        image = image + dot(last[:, start : start + wide], xrecv[h][...].reshape(wide, 1024))
+        start += wide
     for a in range(32):
         out[:, a, :] = jnp.concatenate([image[16 * k : 16 * k + 16, 32 * a : 32 * a + 32] for k in range(4)], axis=1)
 
     pltpu.make_async_copy(csend.at[some], crecv.at[some], cssem).wait()
-    for h in range(CHUNKS):
-        pltpu.make_async_copy(send.at[h, some], recv.at[h, some], ssem).wait()
-        few = pl.ds(0, groups - 1)
-        pltpu.make_async_copy(xsend.at[h, few], xrecv.at[h, few], xssem).wait()
+    for h in range(n):
+        pltpu.make_async_copy(send[h].at[some], recv[h].at[some], ssem.at[h]).wait()
+        pltpu.make_async_copy(xsend[h].at[few], xrecv[h].at[few], xssem.at[h]).wait()
 
 
 def solution(mesh):
     peers, groups = mesh.shape["facet"], mesh.shape["freq"]
     consts = constants()
+    widths = [len(sets) for sets in CHUNKS]
 
     def shards(visibilities, uvw, facet_of, plane_of, cell_of, kernels, centers):
-        vis = jnp.transpose(visibilities[0], (1, 0, 2))
         coords = jnp.transpose(uvw[0], (1, 0, 2))
+        small = [facet_of.reshape(1, -1), plane_of, cell_of, centers.T, coords, visibilities[0], *[jnp.asarray(c) for c in consts]]
         vmem = pl.BlockSpec(memory_space=pltpu.VMEM)
         dma = pltpu.SemaphoreType.DMA
         image = pl.pallas_call(
             functools.partial(kernel, peers, groups),
             out_shape=jax.ShapeDtypeStruct((16, 32, 128), F32),
-            in_specs=[vmem] * 5 + [pl.BlockSpec(memory_space=pl.ANY)] + [vmem] * 6,
+            in_specs=[pl.BlockSpec(memory_space=pltpu.HBM)] * 12,
             out_specs=vmem,
             scratch_shapes=[
+                *[pltpu.VMEM(a.shape, a.dtype) for a in small],
                 pltpu.VMEM((4096, 512), BF16),
                 pltpu.VMEM((4, 256, 128), F32),
                 pltpu.VMEM((512, 4096), BF16),
-                pltpu.VMEM((CHUNKS, 64, SLOTS, 128), BF16),
-                pltpu.VMEM((CHUNKS, 64, SLOTS, 128), BF16),
                 pltpu.VMEM((64, 1, 128), F32),
                 pltpu.VMEM((64, 1, 128), F32),
                 pltpu.VMEM((4, 32, 1024), F32),
                 pltpu.VMEM((2048, 1024), BF16),
-                pltpu.VMEM((2048, 128), F32),
                 pltpu.VMEM((1024, 256), BF16),
-                pltpu.VMEM((CHUNKS, 4, 16, 1024), BF16),
-                pltpu.VMEM((CHUNKS, 4, 16, 1024), BF16),
-                dma, dma, dma((CHUNKS,)), dma, dma, dma, dma((CHUNKS,)),
+                dma((11,)), dma, dma, dma,
+                *[pltpu.VMEM((64, SLOTS, 128 * k), BF16) for k in widths * 2],
+                *[pltpu.VMEM((4, 16 * k, 1024), BF16) for k in widths * 2],
+                *[dma((len(CHUNKS),))] * 4,
+                pltpu.VMEM((2 * SETS, 1024, 128), F32),
             ],
             compiler_params=pltpu.CompilerParams(collective_id=0, has_side_effects=True),
-        )(vis, coords, facet_of.reshape(1, -1), plane_of, cell_of, kernels, centers.T, *[jnp.asarray(c) for c in consts])
+        )(*small, kernels)
         return image.reshape(1, 512, 128)
 
     in_specs = (

time: 57.2 us -> 53.9 us (0.942)
  local copies, waits for them, and re-layouts: 3.55 us -> 1.67 us
  Pallas kernels: 53.4 us -> 52.2 us
    unnamed x2 -> x1, local copies, waits for them, and re-layouts: 3.55 us -> 1.67 us
    pallas_call x1, Pallas kernels: 53.4 us -> 52.2 us  [shards(): pl.pallas_call(functools.partial(kernel, peers, groups), out_shape=jax.Sh...]
where the time goes in v2:
time: 53.9 us; the launch traced here: 53.8 us
  Pallas kernels  52.2 us (97%)
  local copies, waits for them, and re-layouts  1.67 us (3%)
    pallas_call x1, Pallas kernels, shards(): pl.pallas_call(functools.partial(kernel, peers, groups), out_shape=jax.Sh...  52.2 us
    unnamed x1, local copies, waits for them, and re-layouts  1.67 us

profile of v2, /device:TPU:1, one launch (start us, length us, event | category | flops | bytes accessed | tf_op | source)
XLA Modules:
  0.0 53.8 jit_solution(277194984547031797)
XLA Ops:
  0.0 52.2 %shard_map.118 = f32[16,32,128]{2,1,0:T(8,128)} custom-call(s32[1,256]{1,0:T(1,128)} %bitcast.10, s32[1,256]{1,0:T(1,128)} %refs_1_.1, s32[1,256]{1,0:T(1,128)} %refs_2_.1, f32[2,64]{1,0:T(2,128)} %bitcast.11, bf16[3,256,512]{2,1,0:T(8,128)(2,1)} %bitcast.8, bf16[256,2,512]{2,1,0:T(2,128)(2,1)} %bitcast.9, bf16[512,512]{1,0:T(8,128)(2,1)} %constant.10.clone.refs_6_, ...), custom_call_target="tpu_custom_call" | custom-call | tf_op jit(solution)/shard_map/pallas_call | solution.py:295
  52.2 1.7 %copy.14 = f32[1,512,128]{2,1,0:T(8,128)} copy(f32[1,512,128]{2,1,0:T(8,128)} %bitcast.7) | data formatting | bytes 524288

commit v3 on v2

--- a/solution.py
+++ b/solution.py
@@ -14,7 +14,7 @@
 PU_SETS = ((0, 8, 4, 12), (1, 15, 7, 9), (2, 14, 6, 10), (3, 13, 5, 11))
 SETS = 4
 CHUNKS = ((0,), (1,), (2,), (3,))
-AHEAD = 2
+AHEAD = 3
 ROWS = 512
 SINE = (6.283185159611163, -41.34165492934347, 81.60099819261225, -76.54965682060198, 39.53581371130458)
 
@@ -273,13 +273,17 @@
         wide = 64 * len(sets)
         image = image + dot(last[:, start : start + wide], xrecv[h][...].reshape(wide, 1024))
         start += wide
-    for a in range(32):
-        out[:, a, :] = jnp.concatenate([image[16 * k : 16 * k + 16, 32 * a : 32 * a + 32] for k in range(4)], axis=1)
+    out[...] = image
 
     pltpu.make_async_copy(csend.at[some], crecv.at[some], cssem).wait()
     for h in range(n):
         pltpu.make_async_copy(send[h].at[some], recv[h].at[some], ssem.at[h]).wait()
         pltpu.make_async_copy(xsend[h].at[few], xrecv[h].at[few], xssem.at[h]).wait()
+
+
+def settle(image, out):
+    for a in range(32):
+        out[:, a, :] = jnp.concatenate([image[16 * k : 16 * k + 16, 32 * a : 32 * a + 32] for k in range(4)], axis=1)
 
 
 def solution(mesh):
@@ -294,7 +298,7 @@
         dma = pltpu.SemaphoreType.DMA
         image = pl.pallas_call(
             functools.partial(kernel, peers, groups),
-            out_shape=jax.ShapeDtypeStruct((16, 32, 128), F32),
+            out_shape=jax.ShapeDtypeStruct((64, 1024), F32),
             in_specs=[pl.BlockSpec(memory_space=pltpu.HBM)] * 12,
             out_specs=vmem,
             scratch_shapes=[
@@ -315,6 +319,12 @@
             ],
             compiler_params=pltpu.CompilerParams(collective_id=0, has_side_effects=True),
         )(*small, kernels)
+        image = pl.pallas_call(
+            settle,
+            out_shape=jax.ShapeDtypeStruct((16, 32, 128), F32),
+            in_specs=[vmem],
+            out_specs=vmem,
+        )(image)
         return image.reshape(1, 512, 128)
 
     in_specs = (

time: 53.9 us -> 51.4 us (0.954)
  local copies, waits for them, and re-layouts: 1.67 us -> 0 us
  Pallas kernels: 52.2 us -> 51.3 us
    pallas_call x1, Pallas kernels: 52.2 us -> 49.3 us  [shards(): pl.pallas_call(functools.partial(kernel, peers, groups), out_shape=jax.Sh...]
    pallas_call x0 -> x1, Pallas kernels: none -> 2.02 us  [shards(): pl.pallas_call(settle, out_shape=jax.ShapeDtypeStruct((16, 32, 128), F32)...]
    unnamed x1 -> x0, local copies, waits for them, and re-layouts: 1.67 us -> none
where the time goes in v3:
time: 51.4 us; the launch traced here: 51.3 us
  Pallas kernels  51.3 us (100%)
    pallas_call x1, Pallas kernels, shards(): pl.pallas_call(functools.partial(kernel, peers, groups), out_shape=jax.Sh...  49.3 us
    pallas_call x1, Pallas kernels, shards(): pl.pallas_call(settle, out_shape=jax.ShapeDtypeStruct((16, 32, 128), F32)...  2.02 us

profile of v3, /device:TPU:1, one launch (start us, length us, event | category | flops | bytes accessed | tf_op | source)
XLA Modules:
  0.0 51.3 jit_solution(7716800473625265453)
XLA Ops:
  0.0 49.3 %shard_map.118.image = f32[64,1024]{1,0:T(8,128)} custom-call(s32[1,256]{1,0:T(1,128)} %bitcast.9, s32[1,256]{1,0:T(1,128)} %refs_1_.1, s32[1,256]{1,0:T(1,128)} %refs_2_.1, f32[2,64]{1,0:T(2,128)} %bitcast.10, bf16[3,256,512]{2,1,0:T(8,128)(2,1)} %bitcast.7, bf16[256,2,512]{2,1,0:T(2,128)(2,1)} %bitcast.8, bf16[512,512]{1,0:T(8,128)(2,1)} %constant.10.clone.refs_6_, ...), custom_call_target="tpu_custom_call" | custom-call | tf_op jit(solution)/shard_map/pallas_call | solution.py:299
  49.3 2.0 %shard_map.119 = f32[16,32,128]{2,1,0:T(8,128)} custom-call(f32[64,1024]{1,0:T(8,128)} %shard_map.118.image), custom_call_target="tpu_custom_call" | custom-call | tf_op jit(solution)/shard_map/pallas_call | solution.py:322
